TPU v7x, 256 devices: a 8x8x2 block of a 8x8x16 slice. The times are simulated.
256 devices in a mesh: sweep: 2 (over z), expert: 16 (over y, core), fsdp: 8 (over x).
Axes of the slice: x: 8, y: 8, z: 2, core: 2. Of those that a mesh axis runs over, the one named last changes fastest.
The devices are a block of a 8x8x16 slice.
Arguments:
- tokens: bfloat16 [32768, 2048], P(('sweep', 'expert', 'fsdp')), parts along dimension 0, may hold values from -6 to 6
- context: bfloat16 [32768, 2048], P(('sweep', 'expert', 'fsdp')), parts along dimension 0, may hold values from -6 to 6
- out_proj: bfloat16 [4096, 2048], P(('sweep', 'expert', 'fsdp')), parts along dimension 0, may hold values from -0.125 to 0.125
- norm_gain: float32 [4096], P('sweep'), parts along dimension 0, may hold values from 0.1 to 1.9
- router: bfloat16 [4096, 64], P('sweep'), parts along dimension 0, may hold values from -0.125 to 0.125
- expert_ids: int32 [32768, 2], P(('sweep', 'expert', 'fsdp')), parts along dimension 0, may hold values from 0 to 63, all different within a row; in each aligned block of 128 rows (0 to 127, 128 to 255, ...) at most 5 rows name the same one
- w_gate_up: bfloat16 [256, 2, 704, 2048], P(('sweep', 'expert', 'fsdp')), parts along dimension 0, may hold values from -0.125 to 0.125
- w_down: bfloat16 [256, 704, 2048], P(('sweep', 'expert', 'fsdp')), parts along dimension 0, may hold values from -0.15625 to 0.15625
Outputs:
- layer_out: bfloat16 [32768, 2048], P(('sweep', 'expert', 'fsdp')), parts along dimension 0
There are 2 independent parts, one for each index of `sweep`. A program takes and returns all parts, laid end to end along the dimension named above; each array names one. Nothing has to cross between parts.
Inputs may be any that keep to these rules, and one draw needn't show every extreme that they name: `expert_ids`: each row names two different experts. Among the rows of one device no expert is named more than 5 times, a bound that some block reaches.
All inputs are finite; a program needn't handle non-finite values.
Results may differ from a plain program's by a relative error of at most 0.012.
Values may be sent and summed in bfloat16 or wider, within the bound.
A program may use at most 64 MiB of HBM per device.

v0:
```python
import jax
import jax.numpy as jnp
from jax import lax
from jax.sharding import PartitionSpec as P

eps_norm = 1e-05


def half_block(taken, gate_up_w, down_w):
    gate_up = jnp.einsum("rd,kfd->krf", taken, gate_up_w, preferred_element_type=jnp.float32)
    hidden = (jax.nn.silu(gate_up[0]) * gate_up[1]).astype(jnp.bfloat16)
    return jnp.dot(hidden, down_w, preferred_element_type=jnp.float32).astype(jnp.bfloat16)


def slot_places(expert_ids, experts):
    flat_ids = expert_ids.reshape(-1)
    onehot = (flat_ids[:, None] == jnp.arange(experts, dtype=jnp.int32)[None, :]).astype(jnp.int32)
    before = jnp.cumsum(onehot, axis=0) - onehot
    places = jnp.sum(before * onehot, axis=1)
    return (flat_ids, places)


def on_device(tokens, context, out_proj, norm_gain, router, expert_ids, w_gate_up, w_down):
    rows_here, width = tokens.shape
    columns = lax.axis_size("expert")
    members = lax.axis_size("fsdp")
    experts = columns * members // 2
    group = members // 2
    slot_cap = 5 * rows_here // (2 * experts)
    gate_up_here = w_gate_up[0]
    down_here = w_down[0]
    attended = jnp.dot(
        context,
        lax.all_gather(out_proj, ("expert", "fsdp"), axis=0, tiled=True),
        preferred_element_type=jnp.float32,
    )
    residual_in = (tokens.astype(jnp.float32) + attended).astype(jnp.bfloat16)
    widened = residual_in.astype(jnp.float32)
    inv_rms = lax.rsqrt(jnp.mean(widened * widened, axis=1, keepdims=True) + eps_norm)
    normed = (widened * inv_rms * norm_gain).astype(jnp.bfloat16)
    logits = jnp.dot(normed, router, preferred_element_type=jnp.float32)
    picked = jnp.take_along_axis(logits, expert_ids, axis=1)
    scores = jax.nn.sigmoid(picked)
    gate_vals = scores / jnp.sum(scores, axis=1, keepdims=True)
    flat_ids, places = slot_places(expert_ids, experts)
    source_rows = jnp.repeat(normed, 2, axis=0)
    empty_box = jnp.zeros((experts * slot_cap, width), jnp.bfloat16)
    target = (flat_ids % group * columns + flat_ids // group) * slot_cap + places
    outbox = empty_box.at[target].set(source_rows).reshape(group, columns, slot_cap, width)
    arrived = lax.all_to_all(outbox, "expert", split_axis=1, concat_axis=1, tiled=True)
    copies = jnp.repeat(arrived, 2, axis=0)
    pieces = lax.all_to_all(copies, "fsdp", split_axis=0, concat_axis=0, tiled=True)
    slots_in = pieces.shape[2]
    output_half = half_block(
        pieces.reshape(members * columns * slots_in, width), gate_up_here, down_here
    )
    partials = output_half.reshape(members, columns, slots_in, width)
    back = lax.all_to_all(partials, "fsdp", split_axis=0, concat_axis=0, tiled=True)
    halves = back.reshape(group, 2, columns, slot_cap, width).astype(jnp.float32)
    summed = (halves[:, 0] + halves[:, 1]).astype(jnp.bfloat16)
    finished = lax.all_to_all(summed, "expert", split_axis=1, concat_axis=1, tiled=True)
    results = finished.reshape(-1, width)[target].astype(jnp.float32).reshape(rows_here, 2, width)
    output_rows = widened + gate_vals[:, 0:1] * results[:, 0] + gate_vals[:, 1:2] * results[:, 1]
    return output_rows.astype(jnp.bfloat16)


def solution(mesh):
    return jax.shard_map(
        on_device,
        mesh=mesh,
        in_specs=(
            P(("sweep", "expert", "fsdp"), None),
            P(("sweep", "expert", "fsdp"), None),
            P(("sweep", "expert", "fsdp"), None),
            P("sweep"),
            P("sweep", None),
            P(("sweep", "expert", "fsdp"), None),
            P(("sweep", "expert", "fsdp"), None, None, None),
            P(("sweep", "expert", "fsdp"), None, None),
        ),
        out_specs=P(("sweep", "expert", "fsdp"), None),
        check_vma=False,
    )
```

profile of v0, /device:TPU:518, one launch (start us, length us, event | category | flops | bytes accessed | tf_op | source)
XLA Modules:
  0.0 394.7 jit_solution(119510280563451889)
XLA Ops:
  6.5 0.0 copy-start
  6.6 0.7 all-gather.2.cloned.1.call-update
  7.3 0.9 copy.57
  8.2 0.1 eq.31
  8.3 0.1 eq.27
  8.5 0.1 reshape.188
  8.6 0.6 reduce-window.6
  9.3 0.2 slice_reduce_fusion
  9.5 0.1 fusion.22
  9.6 0.0 copy-start.6
  9.6 102.1 %all-gather.2.cloned.1.call-done = bf16[2048,2048]{1,0:T(8,128)(2,1)} async-done(((bf16[16,2048]{1,0:T(8,128)(2,1)}), bf16[2048,2048]{1,0:T(8,128)(2,1)}) %all-gather.2.cloned.1.call-update) | async-done | bytes 8388624 | tf_op jit(solution)/shard_map/all_gather | solution.py:34
  111.7 5.0 %multiply_reduce_fusion = (f32[128]{0:T(128)S(1)}, f32[128,2048]{1,0:T(8,128)S(1)}) fusion(bf16[128,2048]{1,0:T(8,128)(2,1)} %param.9, bf16[2048,2048]{1,0:T(8,128)(2,1)} %all-gather.2.cloned.1.call-done, bf16[128,2048]{1,0:T(8,128)(2,1)} %param.8), kind=kOutput, calls=%fused_computation.24 | convolution fusion | flops 1075314560 | bytes 10486272 | tf_op jit(solution)/shard_map/dot_general | solution.py:32
  116.7 1.0 copy-done.2
  117.6 0.2 multiply_convert_fusion
  117.8 1.7 broadcast_in_dim.21
  119.5 2.3 reshape.216
  121.7 4.0 %scatter_custom_fusion = bf16[320,2048]{1,0:T(8,128)(2,1)} fusion(s32[256]{0:T(256)S(1)} %bitcast.72, bf16[256,2048]{1,0:T(8,128)(2,1)} %reshape.216, bf16[]{:T(256)} %constant.59.clone.1), kind=kCustom, calls=%fused_computation.26 | custom fusion | bytes 1311232 | tf_op jit(solution)/shard_map/scatter | solution.py:49
  125.7 3.4 reshape.191
  129.1 2.9 copy.61
  131.9 38.5 %all_to_all.20 = bf16[4,16,5,2048]{3,0,2,1:T(4,128)(2,1)S(1)} all-to-all(bf16[4,16,5,2048]{3,0,2,1:T(4,128)(2,1)S(1)} %copy.61), channel_id=1, replica_groups=mesh['sweep'=2,'expert'=16,'fsdp'=8] {'expert'}, dimensions={1} | all-to-all | bytes 2621440 | tf_op jit(solution)/shard_map/all_to_all | solution.py:50
  170.5 0.7 copy.62
  171.2 0.3 broadcast_in_dim.22
  171.6 64.8 %all_to_all.21 = bf16[8,16,5,2048]{3,1,2,0:T(8,128)(2,1)S(1)} all-to-all(bf16[8,16,5,2048]{3,1,2,0:T(8,128)(2,1)S(1)} %bitcast.70), channel_id=1, replica_groups=mesh['sweep'=2,'expert'=16,'fsdp'=8] {'fsdp'}, dimensions={0} | all-to-all | bytes 5242880 | tf_op jit(solution)/shard_map/all_to_all | solution.py:52
  236.3 3.6 copy.63
  239.9 5.6 %reshape.225 = bf16[640,2048,1]{1,0,2:T(8,128)(2,1)} reshape(bf16[8,16,5,2048]{3,2,1,0:T(8,128)(2,1)} %copy.63) | data formatting | bytes 5242880 | tf_op jit(solution)/shard_map/reshape | solution.py:55
  245.5 7.5 %fusion.6 = f32[2,640,704]{1,2,0:T(8,128)S(1)} fusion(bf16[640,2048,1]{1,0,2:T(8,128)(2,1)} %reshape.225, bf16[1,2,704,2048]{3,2,1,0:T(8,128)(2,1)} %param.14), kind=kOutput, calls=%fused_computation.12 | convolution fusion | flops 3690987520 | bytes 11993088 | tf_op jit(solution)/shard_map/rd,kfd->krf/dot_general | solution.py:10
  253.0 3.8 convolution_convert_fusion
  256.9 5.5 %reshape.194 = bf16[8,16,5,2048]{3,2,1,0:T(8,128)(2,1)} reshape(bf16[640,2048]{1,0:T(8,128)(2,1)} %convolution_convert_fusion) | data formatting | bytes 5242880 | tf_op jit(solution)/shard_map/reshape | solution.py:57
  262.3 4.1 %copy.64 = bf16[8,16,5,2048]{3,1,2,0:T(8,128)(2,1)S(1)} copy(bf16[8,16,5,2048]{3,2,1,0:T(8,128)(2,1)} %reshape.194) | data formatting | bytes 5242880 | tf_op jit(solution)/shard_map/reshape | solution.py:57
  266.4 65.6 %all_to_all.22 = bf16[8,16,5,2048]{3,1,2,0:T(8,128)(2,1)S(1)} all-to-all(bf16[8,16,5,2048]{3,1,2,0:T(8,128)(2,1)S(1)} %copy.64), channel_id=1, replica_groups=mesh['sweep'=2,'expert'=16,'fsdp'=8] {'fsdp'}, dimensions={0} | all-to-all | bytes 5242880 | tf_op jit(solution)/shard_map/all_to_all | solution.py:58
  332.0 0.7 fusion.28
  332.7 4.1 %fusion.10 = bf16[4,16,5,2048]{3,0,2,1:T(4,128)(2,1)} fusion(f32[4,1,16,5,2048]{4,2,3,1,0:T(8,128)S(1)} %get-tuple-element.8, f32[4,1,16,5,2048]{4,2,3,1,0:T(8,128)S(1)} %get-tuple-element.7), kind=kLoop, calls=%fused_computation.15 | loop fusion | flops 1310720 | bytes 6553600 | tf_op jit(solution)/shard_map/convert_element_type | solution.py:60
  336.9 4.3 %all-to-all-start.3 = ((bf16[4,16,5,2048]{3,0,2,1:T(4,128)(2,1)}), bf16[4,16,5,2048]{3,0,2,1:T(4,128)(2,1)S(1)}, u32[]{:S(2)}, u32[]{:S(2)}) async-start(bf16[4,16,5,2048]{3,0,2,1:T(4,128)(2,1)} %fusion.10), calls=%async_computation.3 | async-start | bytes 2621440 | tf_op jit(solution)/shard_map/all_to_all | solution.py:61
  341.1 0.0 copy-done.5
  341.2 0.1 copy.55
  341.3 0.1 reshape.206
  341.4 0.3 fusion.30
  341.8 2.0 gather_fusion.1
  343.7 0.1 reshape.209
  343.9 0.1 copy.56
  344.0 29.0 %all-to-all-done.3 = bf16[4,16,5,2048]{3,0,2,1:T(4,128)(2,1)S(1)} async-done(((bf16[4,16,5,2048]{3,0,2,1:T(4,128)(2,1)}), bf16[4,16,5,2048]{3,0,2,1:T(4,128)(2,1)S(1)}, u32[]{:S(2)}, u32[]{:S(2)}) %all-to-all-start.3) | async-done | bytes 1310752 | tf_op jit(solution)/shard_map/all_to_all | solution.py:61
  373.0 2.1 copy.67
  375.1 2.6 reshape.195
  377.6 1.4 gather_fusion
  379.0 2.4 reshape.197
  381.4 4.5 %fusion.29 = (f32[128,1,2048]{2,1,0:T(1,128)S(1)}, f32[128,1,2048]{2,1,0:T(1,128)S(1)}) fusion(f32[128,2,2048]{2,1,0:T(2,128)} %reshape.197), kind=kLoop, calls=%fused_computation.58 | loop fusion | bytes 4194304 | tf_op jit(solution)/shard_map/slice | solution.py:63
  385.9 1.9 fusion.13
  387.8 0.0 copy-done.1
  (20 shorter events, 0.2 us)
Async XLA Ops:
  6.5 246.5 %copy-start = (bf16[1,704,2048]{2,1,0:T(8,128)(2,1)S(1)}, bf16[1,704,2048]{2,1,0:T(8,128)(2,1)}, u32[]{:S(2)}) copy-start(bf16[1,704,2048]{2,1,0:T(8,128)(2,1)} %param.15) | copy-start | bytes 8650756
  6.6 105.1 %all-gather.2.cloned.1.call-start = ((), (), s32[]{:S(2)}) async-start(), calls=%async_computation.4 | async-start | bytes 8454144 | tf_op jit(solution)/shard_map/all_gather | solution.py:34
  9.6 108.0 %copy-start.6 = (f32[2048]{0:T(1024)S(1)}, f32[2048]{0:T(1024)}, u32[]{:S(2)}) copy-start(f32[2048]{0:T(1024)} %param.11) | copy-start | bytes 24580
  116.7 1.0 copy-start.2
  336.9 4.3 %copy-start.5 = (s32[128,2]{0,1:T(2,128)S(1)}, s32[128,2]{0,1:T(2,128)}, u32[]{:S(2)}) copy-start(s32[128,2]{0,1:T(2,128)} %param.13) | copy-start | bytes 3076
  336.9 4.6 %copy-start.4 = (bf16[2048,64]{0,1:T(8,128)(2,1)S(1)}, bf16[2048,64]{0,1:T(8,128)(2,1)}, u32[]{:S(2)}) copy-start(bf16[2048,64]{0,1:T(8,128)(2,1)} %param.12) | copy-start | bytes 786436
  336.9 36.1 %all-to-all-start.3 = ((bf16[4,16,5,2048]{3,0,2,1:T(4,128)(2,1)}), bf16[4,16,5,2048]{3,0,2,1:T(4,128)(2,1)S(1)}, u32[]{:S(2)}, u32[]{:S(2)}) async-start(bf16[4,16,5,2048]{3,0,2,1:T(4,128)(2,1)} %fusion.10), calls=%async_computation.3 | async-start | bytes 2621440 | tf_op jit(solution)/shard_map/all_to_all | solution.py:61
  381.4 4.6 %copy-start.3 = (f32[128,2048]{1,0:T(8,128)S(1)}, f32[128,2048]{1,0:T(8,128)}, u32[]{:S(2)}) copy-start(f32[128,2048]{1,0:T(8,128)} %copy-done.2) | copy-start | bytes 3145732
  381.4 6.5 %copy-start.1 = (bf16[1,704,2048]{2,1,0:T(8,128)(2,1)S(1)}, bf16[1,704,2048]{2,1,0:T(8,128)(2,1)}, u32[]{:S(2)}) copy-start(bf16[1,704,2048]{2,1,0:T(8,128)(2,1)} %param.15) | copy-start | bytes 8650756
Sparse Core Ops, SparseCore 0:
  10.0 101.6 all-gather.1
where the time goes:
time: 401 us; the launch traced here: 395 us
  blocking collectives  169 us (42%)
  waiting for transfers between devices  132 us (33%)
  local copies, waits for them, and re-layouts  52.4 us (13%)
  matrix products  16.6 us (4%)
  between operations  13.6 us (3%)
  other arithmetic  7.02 us (2%)
  starting transfers between devices  4.28 us (1%)
    all_gather x1, waiting for transfers between devices, on_device(): lax.all_gather(out_proj, ('expert', 'fsdp'), axis=0, tiled=True)  102 us
    all_to_all x1, blocking collectives, on_device(): lax.all_to_all(partials, 'fsdp', split_axis=0, concat_axis=0, tiled=True)  65.6 us
    all_to_all x1, blocking collectives, on_device(): lax.all_to_all(copies, 'fsdp', split_axis=0, concat_axis=0, tiled=True)  64.8 us
    all_to_all x1, blocking collectives, on_device(): lax.all_to_all(outbox, 'expert', split_axis=1, concat_axis=1, tiled=True)  38.5 us
    all_to_all x1, waiting for transfers between devices, on_device(): lax.all_to_all(summed, 'expert', split_axis=1, concat_axis=1, tiled=True)  29 us
    reshape x2, local copies, waits for them, and re-layouts, on_device(): partials = output_half.reshape(members, columns, slots_in, width)  9.54 us
  transfers between devices with their start and end apart: 2, of which 2 were waited for; matrix products, arithmetic and copies ran while one was open for 1% of the time, Pallas kernels for 0%

commit v1 on v0

v1 whole, which is shorter than its diff:
```python
import functools

import jax
import jax.numpy as jnp
from jax import lax
from jax.experimental import pallas as pl
from jax.experimental.pallas import tpu as pltpu
from jax.sharding import PartitionSpec as P

eps_norm = 1e-05
MESH = pl.DeviceIdType.MESH
f32, bf16 = jnp.float32, jnp.bfloat16


def block_kernel(
    dims,
    tokens_hbm, context_hbm, shard_hbm, gain_ref, router_ref, ids_ref, gate_up_hbm, down_hbm,
    out_ref,
    proj, tok, ctx, resid, normed, gate_up, down,
    slot_rows, pick0, pick1, mask0, mask1,
    wide, outbox, inbox, rows2d, hidden, halves, others, finished,
    load_sem, pair_sem, ring1_send, ring1_recv, ring2_send, ring2_recv, copy_send, copy_recv,
    out_send, out_recv, fwd_send, fwd_recv, half_send, half_recv, home_send, home_recv,
):
    E, F, cap, chunk = dims
    T, D = out_ref.shape
    J = D // 128
    Y, pairs = E // 2, F // 2
    experts = E * pairs
    slots = experts * cap
    rem, div = lax.rem, lax.div

    c = lax.axis_index("expert")
    x = lax.axis_index("fsdp")
    y, core = div(c, 2), rem(c, 2)
    par = rem(x, 2)
    tau = 1 - 2 * par

    def dev(cc, xx):
        return {"expert": cc, "fsdp": xx}

    def wait_bytes(ref, sem):
        pltpu.make_async_copy(ref, ref, sem).wait()

    Dh = D // 2
    loads = [
        pltpu.make_async_copy(shard_hbm.at[:, h * Dh:(h + 1) * Dh], proj.at[h, y, core, x], load_sem.at[h])
        for h in range(2)
    ]
    loads.append(pltpu.make_async_copy(context_hbm, ctx, load_sem.at[2]))
    loads.append(pltpu.make_async_copy(tokens_hbm, tok, load_sem.at[3]))
    loads.append(pltpu.make_async_copy(gate_up_hbm.at[0], gate_up, load_sem.at[4]))
    loads.append(pltpu.make_async_copy(down_hbm.at[0], down, load_sem.at[5]))
    for load in loads:
        load.start()

    barrier = pltpu.get_barrier_semaphore()
    me = c * F + x

    def greet(n, carry):
        other = rem(me + n, E * F)
        pl.semaphore_signal(barrier, inc=1, device_id=dev(div(other, F), rem(other, F)), device_id_type=MESH)
        return carry

    lax.fori_loop(1, E * F, greet, 0)
    pl.semaphore_wait(barrier, E * F - 1)

    loads[0].wait()
    loads[1].wait()
    partner_core = dev(c + 1 - 2 * core, x)
    swap = pltpu.make_async_remote_copy(
        src_ref=proj.at[1 - core, y, core, x], dst_ref=proj.at[1 - core, y, core, x],
        send_sem=pair_sem.at[0], recv_sem=pair_sem.at[1], device_id=partner_core, device_id_type=MESH,
    )
    swap.start()
    own = pltpu.make_async_remote_copy(
        src_ref=proj.at[core, y, core, x], dst_ref=proj.at[core, y, core, x],
        send_sem=pair_sem.at[2], recv_sem=pair_sem.at[3], device_id=partner_core, device_id_type=MESH,
    )
    own.start()
    swap.wait_recv()

    N = F
    pos1 = x * (1 - core) + y * core
    pos2 = y * (1 - core) + x * core

    def piece(p1, p2):
        return proj.at[core, p2 * (1 - core) + p1 * core, :, p1 * (1 - core) + p2 * core]

    def at(p1, p2):
        return dev(2 * (p2 * (1 - core) + p1 * core) + core, p1 * (1 - core) + p2 * core)

    def ring1(way, step, p1):
        sign = 1 - 2 * way
        ref = piece(p1, pos2)
        return pltpu.make_async_remote_copy(
            src_ref=ref, dst_ref=ref, send_sem=ring1_send, recv_sem=ring1_recv.at[way * (N // 2) + step],
            device_id=at(rem(pos1 + sign + N, N), pos2), device_id_type=MESH,
        )

    def ring2(way, step, p1, p2, o):
        sign = 1 - 2 * way
        ref = piece(p1, p2)
        return pltpu.make_async_remote_copy(
            src_ref=ref, dst_ref=ref, send_sem=ring2_send,
            recv_sem=ring2_recv.at[(way * (N // 2) + step) * N + o],
            device_id=at(pos1, rem(pos2 + sign + N, N)), device_id_type=MESH,
        )

    def to_partner(p1, p2, which):
        ref = piece(p1, p2)
        return pltpu.make_async_remote_copy(
            src_ref=ref, dst_ref=ref, send_sem=copy_send.at[which], recv_sem=copy_recv.at[which],
            device_id=partner_core, device_id_type=MESH,
        )

    ring1(0, 0, pos1).start()
    ring1(1, 0, pos1).start()
    ring2(0, 0, pos1, pos2, 0).start()
    ring2(1, 0, pos1, pos2, 0).start()

    ids = ids_ref[...]
    expert_row = lax.broadcasted_iota(jnp.int32, (experts, T), 0)
    one0 = (expert_row == ids[0:1, :]).astype(f32)
    one1 = (expert_row == ids[1:2, :]).astype(f32)
    earlier = (
        lax.broadcasted_iota(jnp.int32, (T, T), 0) < lax.broadcasted_iota(jnp.int32, (T, T), 1)
    ).astype(bf16)
    before = jnp.dot((one0 + one1).astype(bf16), earlier, preferred_element_type=f32)
    place0 = jnp.sum(before * one0, axis=0, keepdims=True).astype(jnp.int32)
    place1 = jnp.sum(before * one1, axis=0, keepdims=True).astype(jnp.int32)
    slot_row = lax.broadcasted_iota(jnp.int32, (slots, T), 0)
    sel0 = (slot_row == ids[0:1, :] * cap + place0).astype(f32)
    sel1 = (slot_row == ids[1:2, :] * cap + place1).astype(f32)
    slot_rows[...] = (sel0 + sel1).astype(bf16)
    pick0[...] = jnp.transpose(sel0).astype(bf16)
    pick1[...] = jnp.transpose(sel1).astype(bf16)
    mask0[...] = jnp.transpose(one0)
    mask1[...] = jnp.transpose(one1)

    for step in range(1, N // 2 + 1):
        for way in range(2):
            if way == 1 and step == N // 2:
                continue
            sign = 1 - 2 * way
            p1 = rem(pos1 - sign * step + N, N)
            o = 2 * step - 1 + way
            ring1(way, step - 1, p1).wait_recv()
            if step < N // 2 - way:
                ring1(way, step, p1).start()
            ring2(0, 0, p1, pos2, o).start()
            ring2(1, 0, p1, pos2, o).start()
            to_partner(p1, pos2, 0).start()

    for step in range(1, N // 2 + 1):

        def pass_on(oo, carry, step=step):
            for odd in range(2):
                o = 2 * oo + odd
                half = div(o + 1, 2)
                p1 = rem(pos1 + (half if odd == 0 else -half) + N, N)
                for way in range(2):
                    hops = N // 2 if way == odd else N // 2 - 1
                    if step > hops:
                        continue
                    sign = 1 - 2 * way
                    p2 = rem(pos2 - sign * step + N, N)
                    ring2(way, step - 1, p1, p2, o).wait_recv()
                    if step < hops:
                        ring2(way, step, p1, p2, o).start()
                    to_partner(p1, p2, 1).start()
            return carry

        lax.fori_loop(0, N // 2, pass_on, 0)

    own.wait_recv()
    wait_bytes(proj.at[1 - core, pl.ds(0, 1), :, pl.ds(0, N - 1)], copy_recv.at[0])
    wait_bytes(proj.at[1 - core, pl.ds(0, N - 1)], copy_recv.at[1])

    loads[2].wait()
    loads[3].wait()
    wide_cols = 512 if D >= 2048 else 128
    squares = jnp.zeros((T, 1), f32)
    for n in range(D // wide_cols):
        at_col = n * wide_cols
        h, off = at_col // Dh, at_col % Dh
        weights = proj[h, :, :, :, :, off:off + wide_cols].reshape(D, wide_cols)
        attended = jnp.dot(ctx[...], weights, preferred_element_type=f32)
        cols = slice(at_col, at_col + wide_cols)
        r = (tok[:, cols].astype(f32) + attended).astype(bf16)
        resid[:, cols] = r
        r = r.astype(f32)
        squares = squares + jnp.sum(r * r, axis=1, keepdims=True)
    inv_rms = lax.rsqrt(squares * (1.0 / D) + eps_norm)
    for n in range(D // wide_cols):
        cols = slice(n * wide_cols, (n + 1) * wide_cols)
        normed[:, cols] = (resid[:, cols].astype(f32) * inv_rms * gain_ref[:, cols]).astype(bf16)

    for jj in range(J // 2):
        cols = slice(256 * jj, 256 * jj + 256)
        got = jnp.dot(slot_rows[...], normed[:, cols], preferred_element_type=f32)
        wide[0:slots, 2 * jj, :] = got[:, :128]
        wide[0:slots, 2 * jj + 1, :] = got[:, 128:]
    eb = 4

    def narrow(n, carry):
        block = wide[pl.ds(n * eb * cap, eb * cap)].astype(bf16)
        outbox[pl.ds(n * eb, eb)] = block.reshape(eb, cap, J, 128)
        return carry

    lax.fori_loop(0, experts // eb, narrow, 0)

    def shift(k):
        return div(k + 1, 2) * rem(k, 2) + rem(E - div(k, 2), E) * (1 - rem(k, 2))

    def near(i):
        return rem(x + tau * (i if i % 2 == 0 else -i) + F, F)

    def send_slot(k, i):
        to_c, to_x = rem(c + shift(k), E), near(i)
        return pltpu.make_async_remote_copy(
            src_ref=outbox.at[pairs * to_c + div(to_x, 2)], dst_ref=inbox.at[c, rem(to_x, 2), i],
            send_sem=out_send, recv_sem=out_recv.at[k], device_id=dev(to_c, to_x), device_id_type=MESH,
        )

    for i in range(pairs - 1, 0, -1):
        send_slot(0, i).start()
    inbox[c, par, 0] = outbox[pairs * c + div(x, 2)]

    def send_round(k, carry):
        for i in range(pairs - 1, -1, -1):
            send_slot(k, i).start()
        return carry

    lax.fori_loop(1, E, send_round, 0)

    logits = lax.dot_general(
        normed[...], router_ref[...], (((1,), (1,)), ((), ())), preferred_element_type=f32
    )
    score0 = 1.0 / (1.0 + jnp.exp(-jnp.sum(logits * mask0[...], axis=1, keepdims=True)))
    score1 = 1.0 / (1.0 + jnp.exp(-jnp.sum(logits * mask1[...], axis=1, keepdims=True)))
    gate0 = score0 / (score0 + score1)
    gate1 = score1 / (score0 + score1)

    partner = dev(c, x + tau)

    def source(k):
        return rem(c + E - shift(k), E)

    def forward(k):
        ref = inbox.at[source(k), par]
        return pltpu.make_async_remote_copy(
            src_ref=ref, dst_ref=ref, send_sem=fwd_send, recv_sem=fwd_recv.at[k],
            device_id=partner, device_id_type=MESH,
        )

    def pump(g):
        def one(kk, carry):
            k = g * chunk + kk
            wait_bytes(inbox.at[0, 0], out_recv.at[k])
            forward(k).start()
            return carry

        lax.fori_loop(0, chunk, one, 0)

    def pump_first():
        wait_bytes(inbox.at[0, 0, pl.ds(0, pairs - 1)], out_recv.at[0])
        forward(0).start()

        def one(k, carry):
            wait_bytes(inbox.at[0, 0], out_recv.at[k])
            forward(k).start()
            return carry

        lax.fori_loop(1, chunk, one, 0)

    per = 2 * pairs * cap
    rows = chunk * per

    def half_back(k):
        src = source(k)
        return pltpu.make_async_remote_copy(
            src_ref=halves.at[src, 1 - par], dst_ref=others.at[src], send_sem=half_send, recv_sem=half_recv.at[k],
            device_id=partner, device_id_type=MESH,
        )

    def experts_on(g):
        def take(kk, carry):
            k = g * chunk + kk
            wait_bytes(inbox.at[0, 0], fwd_recv.at[k])
            block = inbox[source(k)].reshape(per, J, 128)
            wide[pl.ds(kk * per, per)] = block.astype(f32)
            return carry

        lax.fori_loop(0, chunk, take, 0)
        for jj in range(J // 2):
            both = jnp.concatenate([wide[0:rows, 2 * jj, :], wide[0:rows, 2 * jj + 1, :]], axis=1)
            rows2d[:, 256 * jj:256 * jj + 256] = both.astype(bf16)
        over_last = (((1,), (1,)), ((), ()))
        gate = lax.dot_general(rows2d[...], gate_up[0], over_last, preferred_element_type=f32)
        up = lax.dot_general(rows2d[...], gate_up[1], over_last, preferred_element_type=f32)
        hidden[...] = (gate / (1.0 + jnp.exp(-gate)) * up).astype(bf16)
        for jj in range(J // 2):
            got = jnp.dot(hidden[...], down[:, 256 * jj:256 * jj + 256], preferred_element_type=f32)
            wide[0:rows, 2 * jj, :] = got[:, :128]
            wide[0:rows, 2 * jj + 1, :] = got[:, 128:]

        def give(kk, carry):
            k = g * chunk + kk
            block = wide[pl.ds(kk * per, per)].astype(bf16)
            halves[source(k)] = block.reshape(2, pairs, cap, J, 128)
            half_back(k).start()
            return carry

        lax.fori_loop(0, chunk, give, 0)

    mine = pairs * c + div(x, 2)

    def send_home(k, i):
        src = source(k)
        return pltpu.make_async_remote_copy(
            src_ref=halves.at[src, par, i], dst_ref=finished.at[mine], send_sem=home_send, recv_sem=home_recv,
            device_id=dev(src, rem(x - tau * i + F, F)), device_id_type=MESH,
        )

    def add_halves(k):
        src = source(k)
        wait_bytes(others.at[0], half_recv.at[k])
        total = halves[src, par].astype(f32) + others[src].astype(f32)
        halves[src, par] = total.astype(bf16)

    def finish(g):
        def one(kk, carry):
            k = g * chunk + kk
            add_halves(k)
            for i in range(pairs - 1, -1, -1):
                send_home(k, i).start()
            return carry

        lax.fori_loop(0, chunk, one, 0)

    def finish_first():
        add_halves(0)
        for i in range(pairs - 1, 0, -1):
            send_home(0, i).start()
        finished[mine] = halves[c, par, 0]

        def one(k, carry):
            add_halves(k)
            for i in range(pairs - 1, -1, -1):
                send_home(k, i).start()
            return carry

        lax.fori_loop(1, chunk, one, 0)

    loads[4].wait()
    loads[5].wait()
    groups = E // chunk
    pump_first()
    pump(1)
    experts_on(0)
    pump(2)
    experts_on(1)
    finish_first()

    def middle(g, carry):
        pump(g + 1)
        experts_on(g)
        finish(g - 1)
        return carry

    lax.fori_loop(2, groups - 1, middle, 0)
    experts_on(groups - 1)
    finish(groups - 2)
    finish(groups - 1)

    wait_bytes(finished.at[pl.ds(0, experts - 1)], home_recv)

    def widen(n, carry):
        block = finished[pl.ds(n * eb, eb)].astype(f32)
        wide[pl.ds(n * eb * cap, eb * cap)] = block.reshape(eb * cap, J, 128)
        return carry

    lax.fori_loop(0, experts // eb, widen, 0)
    for jj in range(J // 2):
        cols = slice(256 * jj, 256 * jj + 256)
        got = jnp.concatenate([wide[0:slots, 2 * jj, :], wide[0:slots, 2 * jj + 1, :]], axis=1).astype(bf16)
        first = jnp.dot(pick0[...], got, preferred_element_type=f32)
        second = jnp.dot(pick1[...], got, preferred_element_type=f32)
        out_ref[:, cols] = (resid[:, cols].astype(f32) + gate0 * first + gate1 * second).astype(bf16)

    swap.wait_send()
    own.wait_send()
    wait_bytes(proj.at[core, pl.ds(0, 1), :, pl.ds(0, N - 1)], ring1_send)
    wait_bytes(proj.at[core, pl.ds(0, N - 1)], ring2_send)
    wait_bytes(proj.at[core, pl.ds(0, 1), :, pl.ds(0, N - 1)], copy_send.at[0])
    wait_bytes(proj.at[core, pl.ds(0, N - 1)], copy_send.at[1])
    wait_bytes(outbox.at[pl.ds(0, experts - 1)], out_send)
    wait_bytes(inbox.at[:, 0], fwd_send)
    wait_bytes(others, half_send)
    wait_bytes(finished.at[pl.ds(0, experts - 1)], home_send)


def on_device(tokens, context, out_proj, norm_gain, router, expert_ids, w_gate_up, w_down):
    T, D = tokens.shape
    E, F = lax.axis_size("expert"), lax.axis_size("fsdp")
    Y, pairs = E // 2, F // 2
    experts = E * pairs
    cap = 5 * T // (2 * experts)
    J = D // 128
    R = out_proj.shape[0]
    half_units = w_down.shape[1]
    slots = experts * cap
    chunk = E // 4
    rows = chunk * 2 * pairs * cap
    N = F
    vmem, dma = pltpu.VMEM, pltpu.SemaphoreType.DMA
    any_space = pl.BlockSpec(memory_space=pl.ANY)
    in_vmem = pl.BlockSpec(memory_space=pltpu.VMEM)
    return pl.pallas_call(
        functools.partial(block_kernel, (E, F, cap, chunk)),
        out_shape=jax.ShapeDtypeStruct((T, D), bf16),
        in_specs=[any_space, any_space, any_space, in_vmem, in_vmem, in_vmem, any_space, any_space],
        out_specs=in_vmem,
        scratch_shapes=[
            vmem((2, Y, 2, F, R, D // 2), bf16),
            vmem((T, D), bf16), vmem((T, D), bf16), vmem((T, D), bf16), vmem((T, D), bf16),
            vmem((2, half_units, D), bf16), vmem((half_units, D), bf16),
            vmem((slots, T), bf16), vmem((T, slots), bf16), vmem((T, slots), bf16),
            vmem((T, experts), f32), vmem((T, experts), f32),
            vmem((max(slots, rows), J, 128), f32),
            vmem((experts, cap, J, 128), bf16),
            vmem((E, 2, pairs, cap, J, 128), bf16),
            vmem((rows, D), bf16), vmem((rows, half_units), bf16),
            vmem((E, 2, pairs, cap, J, 128), bf16),
            vmem((E, pairs, cap, J, 128), bf16),
            vmem((experts, cap, J, 128), bf16),
            dma((6,)), dma((4,)), dma, dma((N,)), dma, dma((N * N,)), dma((2,)), dma((2,)),
            dma, dma((E,)), dma, dma((E,)), dma, dma((E,)), dma, dma,
        ],
        compiler_params=pltpu.CompilerParams(
            collective_id=0, has_side_effects=True, vmem_limit_bytes=56 * 1024 * 1024
        ),
        name="block",
    )(
        tokens, context, out_proj, norm_gain.reshape(1, D), router.T, expert_ids.T, w_gate_up, w_down
    )


def solution(mesh):
    return jax.shard_map(
        on_device,
        mesh=mesh,
        in_specs=(
            P(("sweep", "expert", "fsdp"), None),
            P(("sweep", "expert", "fsdp"), None),
            P(("sweep", "expert", "fsdp"), None),
            P("sweep"),
            P("sweep", None),
            P(("sweep", "expert", "fsdp"), None),
            P(("sweep", "expert", "fsdp"), None, None, None),
            P(("sweep", "expert", "fsdp"), None, None),
        ),
        out_specs=P(("sweep", "expert", "fsdp"), None),
        check_vma=False,
    )
```

time: 401 us -> 169 us (0.42); the launches traced: 395 us -> 167 us
  blocking collectives: 169 us -> 0 us
  Pallas kernels: 0 us -> 166 us
  waiting for transfers between devices: 132 us -> 0 us
  local copies, waits for them, and re-layouts: 52.4 us -> 1.88 us
  matrix products: 16.6 us -> 0 us
  between operations: 13.6 us -> 0.01 us
  other arithmetic: 7.02 us -> 0 us
  starting transfers between devices: 4.28 us -> 0 us
    all_to_all x3 -> x0, blocking collectives: 169 us -> none  [the longest x1 65.6 us: on_device(): lax.all_to_all(partials, 'fsdp', split_axis=0, concat_axis=0, tiled=True)]
    pallas_call x0 -> x1, Pallas kernels: none -> 166 us  [on_device(): pl.pallas_call(functools.partial(block_kernel, (E, F, cap, chunk)), out_s...]
    all_gather x1 -> x0, waiting for transfers between devices: 102 us -> none  [on_device(): lax.all_gather(out_proj, ('expert', 'fsdp'), axis=0, tiled=True)]
    all_to_all x1 -> x0, waiting for transfers between devices: 29 us -> none  [on_device(): lax.all_to_all(summed, 'expert', split_axis=1, concat_axis=1, tiled=True)]
    reshape x8 -> x0, local copies, waits for them, and re-layouts: 26.3 us -> none  [the longest x2 9.54 us: on_device(): partials = output_half.reshape(members, columns, slots_in, width)]
    dot_general x4 -> x0, matrix products: 16.6 us -> none  [the longest x1 7.52 us: half_block(): jnp.einsum('rd,kfd->krf', taken, gate_up_w, preferred_element_type=jnp.fl...]
    all_to_all x3 -> x0, local copies, waits for them, and re-layouts: 6.38 us -> none  [the longest x1 3.56 us: on_device(): lax.all_to_all(copies, 'fsdp', split_axis=0, concat_axis=0, tiled=True)]
    convert_element_type x4 -> x0, other arithmetic: 6.17 us -> none  [the longest x1 4.11 us: on_device(): summed = (halves[:, 0] + halves[:, 1]).astype(jnp.bfloat16)]
  transfers between devices with their start and end apart: 2 -> 0, of which waited for: 2 -> 0; matrix products, arithmetic and copies ran while one was open for 1% -> 0% of each run, Pallas kernels for 0% -> 0%
where the time goes in v1:
time: 169 us; the launch traced here: 167 us
  Pallas kernels  166 us (98%)
  local copies, waits for them, and re-layouts  1.88 us (1%)
    pallas_call x1, Pallas kernels, on_device(): pl.pallas_call(functools.partial(block_kernel, (E, F, cap, chunk)), out_s...  166 us

profile of v1, /device:TPU:518, one launch (start us, length us, event | category | flops | bytes accessed | tf_op | source)
XLA Modules:
  0.0 167.4 jit_solution(912457683065319211)
XLA Ops:
  0.0 165.5 %block.1 = bf16[128,2048]{1,0:T(8,128)(2,1)} custom-call(bf16[128,2048]{1,0:T(8,128)(2,1)} %tokens_hbm.1, bf16[128,2048]{1,0:T(8,128)(2,1)} %context_hbm.1, bf16[16,2048]{1,0:T(8,128)(2,1)} %shard_hbm.1, f32[1,2048]{1,0:T(1,128)} %bitcast.4, bf16[64,2048]{1,0:T(8,128)(2,1)} %bitcast.3, s32[2,128]{1,0:T(2,128)} %bitcast.5, ...), custom_call_target="tpu_custom_call" | custom-call | tf_op jit(solution)/shard_map/block/pallas_call | solution.py:420
  165.6 1.9 %copy.10 = bf16[128,2048]{1,0:T(8,128)(2,1)} copy(bf16[128,2048]{1,0:T(8,128)(2,1)} %block.1) | data formatting | bytes 1048576

commit v2 on v1

--- a/solution.py
+++ b/solution.py
@@ -17,7 +17,7 @@
     tokens_hbm, context_hbm, shard_hbm, gain_ref, router_ref, ids_ref, gate_up_hbm, down_hbm,
     out_ref,
     proj, tok, ctx, resid, normed, gate_up, down,
-    slot_rows, pick0, pick1, mask0, mask1,
+    slot_rows, picks, mask0, mask1, total,
     wide, outbox, inbox, rows2d, hidden, halves, others, finished,
     load_sem, pair_sem, ring1_send, ring1_recv, ring2_send, ring2_recv, copy_send, copy_recv,
     out_send, out_recv, fwd_send, fwd_recv, half_send, half_recv, home_send, home_recv,
@@ -54,20 +54,17 @@
     for load in loads:
         load.start()
 
+    N = F
+    partner_core = dev(c + 1 - 2 * core, x)
+    first = [partner_core]
+    first += [dev(c, rem(x + n, F)) for n in (1, F - 1)] + [dev(rem(c + n, E), x) for n in (2, E - 2)]
     barrier = pltpu.get_barrier_semaphore()
-    me = c * F + x
-
-    def greet(n, carry):
-        other = rem(me + n, E * F)
-        pl.semaphore_signal(barrier, inc=1, device_id=dev(div(other, F), rem(other, F)), device_id_type=MESH)
-        return carry
-
-    lax.fori_loop(1, E * F, greet, 0)
-    pl.semaphore_wait(barrier, E * F - 1)
+    for other in first:
+        pl.semaphore_signal(barrier, inc=1, device_id=other, device_id_type=MESH)
+    pl.semaphore_wait(barrier, len(first))
 
     loads[0].wait()
     loads[1].wait()
-    partner_core = dev(c + 1 - 2 * core, x)
     swap = pltpu.make_async_remote_copy(
         src_ref=proj.at[1 - core, y, core, x], dst_ref=proj.at[1 - core, y, core, x],
         send_sem=pair_sem.at[0], recv_sem=pair_sem.at[1], device_id=partner_core, device_id_type=MESH,
@@ -80,7 +77,6 @@
     own.start()
     swap.wait_recv()
 
-    N = F
     pos1 = x * (1 - core) + y * core
     pos2 = y * (1 - core) + x * core
 
@@ -114,10 +110,10 @@
             device_id=partner_core, device_id_type=MESH,
         )
 
-    ring1(0, 0, pos1).start()
-    ring1(1, 0, pos1).start()
     ring2(0, 0, pos1, pos2, 0).start()
     ring2(1, 0, pos1, pos2, 0).start()
+    for way in range(2):
+        ring1(way, 0, pos1).start()
 
     ids = ids_ref[...]
     expert_row = lax.broadcasted_iota(jnp.int32, (experts, T), 0)
@@ -133,64 +129,69 @@
     sel0 = (slot_row == ids[0:1, :] * cap + place0).astype(f32)
     sel1 = (slot_row == ids[1:2, :] * cap + place1).astype(f32)
     slot_rows[...] = (sel0 + sel1).astype(bf16)
-    pick0[...] = jnp.transpose(sel0).astype(bf16)
-    pick1[...] = jnp.transpose(sel1).astype(bf16)
+    expert = lax.broadcasted_iota(jnp.int32, (experts, 1), 0)
+    ahead = jnp.right_shift(expert, pairs.bit_length() - 1) - c
+    ahead = jnp.where(ahead < 0, ahead + E, ahead)
+    turn_of = jnp.where(ahead > E // 2, 2 * (E - ahead), 2 * ahead - jnp.minimum(ahead, 1))
+    start = (turn_of * (pairs * cap) + jnp.bitwise_and(expert, pairs - 1) * cap).astype(f32)
+    home0 = jnp.sum((before + start) * one0, axis=0, keepdims=True).astype(jnp.int32)
+    home1 = jnp.sum((before + start) * one1, axis=0, keepdims=True).astype(jnp.int32)
+    part = chunk * pairs * cap
+    for n, home in enumerate((home0, home1)):
+        chosen = jnp.transpose((slot_row == home).astype(f32)).astype(bf16)
+        for g in range(E // chunk):
+            picks[g, n * T:(n + 1) * T, :] = chosen[:, g * part:(g + 1) * part]
     mask0[...] = jnp.transpose(one0)
     mask1[...] = jnp.transpose(one1)
 
-    for step in range(1, N // 2 + 1):
+    def pass_on(o, step):
+        p1 = rem(pos1 + (o // 2 if o % 2 == 0 else N - (o + 1) // 2), N)
         for way in range(2):
-            if way == 1 and step == N // 2:
+            hops = N // 2 if way == o % 2 else N // 2 - 1
+            if step > hops:
                 continue
-            sign = 1 - 2 * way
-            p1 = rem(pos1 - sign * step + N, N)
-            o = 2 * step - 1 + way
-            ring1(way, step - 1, p1).wait_recv()
-            if step < N // 2 - way:
-                ring1(way, step, p1).start()
-            ring2(0, 0, p1, pos2, o).start()
-            ring2(1, 0, p1, pos2, o).start()
-            to_partner(p1, pos2, 0).start()
-
-    for step in range(1, N // 2 + 1):
-
-        def pass_on(oo, carry, step=step):
-            for odd in range(2):
-                o = 2 * oo + odd
-                half = div(o + 1, 2)
-                p1 = rem(pos1 + (half if odd == 0 else -half) + N, N)
-                for way in range(2):
-                    hops = N // 2 if way == odd else N // 2 - 1
-                    if step > hops:
-                        continue
-                    sign = 1 - 2 * way
-                    p2 = rem(pos2 - sign * step + N, N)
-                    ring2(way, step - 1, p1, p2, o).wait_recv()
-                    if step < hops:
-                        ring2(way, step, p1, p2, o).start()
-                    to_partner(p1, p2, 1).start()
-            return carry
-
-        lax.fori_loop(0, N // 2, pass_on, 0)
-
-    own.wait_recv()
-    wait_bytes(proj.at[1 - core, pl.ds(0, 1), :, pl.ds(0, N - 1)], copy_recv.at[0])
-    wait_bytes(proj.at[1 - core, pl.ds(0, N - 1)], copy_recv.at[1])
+            p2 = rem(pos2 + (N - step if way == 0 else step), N)
+            ring2(way, step - 1, p1, p2, o).wait_recv()
+            if step < hops:
+                ring2(way, step, p1, p2, o).start()
+            to_partner(p1, p2, 1).start()
+
+    for slot in range(1, N + 1):
+        if slot <= N // 2:
+            for way in range(2):
+                if way == 1 and slot == N // 2:
+                    continue
+                p1 = rem(pos1 + (N - slot if way == 0 else slot), N)
+                o = 2 * slot - 1 + way
+                ring1(way, slot - 1, p1).wait_recv()
+                if slot < N // 2 - way:
+                    ring1(way, slot, p1).start()
+                ring2(0, 0, p1, pos2, o).start()
+                ring2(1, 0, p1, pos2, o).start()
+                to_partner(p1, pos2, 0).start()
+        for o in range(N):
+            step = slot - (o + 1) // 2
+            if 1 <= step <= N // 2:
+                pass_on(o, step)
 
     loads[2].wait()
     loads[3].wait()
     wide_cols = 512 if D >= 2048 else 128
     squares = jnp.zeros((T, 1), f32)
-    for n in range(D // wide_cols):
-        at_col = n * wide_cols
-        h, off = at_col // Dh, at_col % Dh
-        weights = proj[h, :, :, :, :, off:off + wide_cols].reshape(D, wide_cols)
-        attended = jnp.dot(ctx[...], weights, preferred_element_type=f32)
-        cols = slice(at_col, at_col + wide_cols)
-        r = (tok[:, cols].astype(f32) + attended).astype(bf16)
-        resid[:, cols] = r
-        r = r.astype(f32)
-        squares = squares + jnp.sum(r * r, axis=1, keepdims=True)
+    for turn in range(2):
+        h = core if turn == 0 else 1 - core
+        if turn == 1:
+            own.wait_recv()
+            wait_bytes(proj.at[1 - core, pl.ds(0, 1), :, pl.ds(0, N - 1)], copy_recv.at[0])
+            wait_bytes(proj.at[1 - core, pl.ds(0, N - 1)], copy_recv.at[1])
+        for off in range(0, Dh, wide_cols):
+            weights = proj[h, :, :, :, :, off:off + wide_cols].reshape(D, wide_cols)
+            attended = jnp.dot(ctx[...], weights, preferred_element_type=f32)
+            cols = pl.ds(pl.multiple_of(h * Dh + off, wide_cols), wide_cols)
+            r = (tok[:, cols].astype(f32) + attended).astype(bf16)
+            resid[:, cols] = r
+            r = r.astype(f32)
+            squares = squares + jnp.sum(r * r, axis=1, keepdims=True)
     inv_rms = lax.rsqrt(squares * (1.0 / D) + eps_norm)
     for n in range(D // wide_cols):
         cols = slice(n * wide_cols, (n + 1) * wide_cols)
@@ -309,25 +310,27 @@
             k = g * chunk + kk
             block = wide[pl.ds(kk * per, per)].astype(bf16)
             halves[source(k)] = block.reshape(2, pairs, cap, J, 128)
-            half_back(k).start()
+            if g > 0:
+                half_back(k).start()
             return carry
 
         lax.fori_loop(0, chunk, give, 0)
 
-    mine = pairs * c + div(x, 2)
+    mine = div(x, 2)
 
     def send_home(k, i):
         src = source(k)
         return pltpu.make_async_remote_copy(
-            src_ref=halves.at[src, par, i], dst_ref=finished.at[mine], send_sem=home_send, recv_sem=home_recv,
+            src_ref=halves.at[src, par, i], dst_ref=finished.at[k, mine], send_sem=home_send,
+            recv_sem=home_recv.at[k],
             device_id=dev(src, rem(x - tau * i + F, F)), device_id_type=MESH,
         )
 
     def add_halves(k):
         src = source(k)
         wait_bytes(others.at[0], half_recv.at[k])
-        total = halves[src, par].astype(f32) + others[src].astype(f32)
-        halves[src, par] = total.astype(bf16)
+        both = halves[src, par].astype(f32) + others[src].astype(f32)
+        halves[src, par] = both.astype(bf16)
 
     def finish(g):
         def one(kk, carry):
@@ -343,7 +346,7 @@
         add_halves(0)
         for i in range(pairs - 1, 0, -1):
             send_home(0, i).start()
-        finished[mine] = halves[c, par, 0]
+        finished[0, mine] = halves[c, par, 0]
 
         def one(k, carry):
             add_halves(k)
@@ -356,38 +359,48 @@
     loads[4].wait()
     loads[5].wait()
     groups = E // chunk
+
+    def go_back(k, carry):
+        half_back(k).start()
+        return carry
+
     pump_first()
     pump(1)
-    experts_on(0)
-    pump(2)
-    experts_on(1)
+    for g in range(groups):
+        if g + 2 < groups:
+            pump(g + 2)
+        experts_on(g)
+        if g == groups - 1:
+            lax.fori_loop(0, chunk, go_back, 0)
+        if g > 1:
+            finish(g - 1)
+
+    finish(groups - 1)
     finish_first()
 
-    def middle(g, carry):
-        pump(g + 1)
-        experts_on(g)
-        finish(g - 1)
+    def widen(k):
+        wide[pl.ds(rem(k, chunk) * pairs * cap, pairs * cap)] = finished[k].reshape(pairs * cap, J, 128).astype(f32)
+
+    def arrived(k, carry):
+        wait_bytes(finished.at[0], home_recv.at[k])
+        widen(k)
         return carry
 
-    lax.fori_loop(2, groups - 1, middle, 0)
-    experts_on(groups - 1)
-    finish(groups - 2)
-    finish(groups - 1)
-
-    wait_bytes(finished.at[pl.ds(0, experts - 1)], home_recv)
-
-    def widen(n, carry):
-        block = finished[pl.ds(n * eb, eb)].astype(f32)
-        wide[pl.ds(n * eb * cap, eb * cap)] = block.reshape(eb * cap, J, 128)
-        return carry
-
-    lax.fori_loop(0, experts // eb, widen, 0)
-    for jj in range(J // 2):
-        cols = slice(256 * jj, 256 * jj + 256)
-        got = jnp.concatenate([wide[0:slots, 2 * jj, :], wide[0:slots, 2 * jj + 1, :]], axis=1).astype(bf16)
-        first = jnp.dot(pick0[...], got, preferred_element_type=f32)
-        second = jnp.dot(pick1[...], got, preferred_element_type=f32)
-        out_ref[:, cols] = (resid[:, cols].astype(f32) + gate0 * first + gate1 * second).astype(bf16)
+    for g in list(range(1, groups)) + [0]:
+        if g == 0:
+            wait_bytes(finished.at[0, pl.ds(0, pairs - 1)], home_recv.at[0])
+            widen(0)
+        lax.fori_loop(max(1, g * chunk), (g + 1) * chunk, arrived, 0)
+        for jj in range(J // 2):
+            cols = slice(256 * jj, 256 * jj + 256)
+            got = jnp.concatenate([wide[0:part, 2 * jj, :], wide[0:part, 2 * jj + 1, :]], axis=1).astype(bf16)
+            picked = jnp.dot(picks[g], got, preferred_element_type=f32)
+            so_far = resid[:, cols].astype(f32) if g == 1 else total[:, cols]
+            so_far = so_far + gate0 * picked[:T] + gate1 * picked[T:]
+            if g > 0:
+                total[:, cols] = so_far
+            else:
+                out_ref[:, cols] = so_far.astype(bf16)
 
     swap.wait_send()
     own.wait_send()
@@ -398,7 +411,7 @@
     wait_bytes(outbox.at[pl.ds(0, experts - 1)], out_send)
     wait_bytes(inbox.at[:, 0], fwd_send)
     wait_bytes(others, half_send)
-    wait_bytes(finished.at[pl.ds(0, experts - 1)], home_send)
+    wait_bytes(outbox.at[pl.ds(0, experts - 1)], home_send)
 
 
 def on_device(tokens, context, out_proj, norm_gain, router, expert_ids, w_gate_up, w_down):
@@ -419,24 +432,24 @@
     in_vmem = pl.BlockSpec(memory_space=pltpu.VMEM)
     return pl.pallas_call(
         functools.partial(block_kernel, (E, F, cap, chunk)),
-        out_shape=jax.ShapeDtypeStruct((T, D), bf16),
+        out_shape=pltpu.VMEM((T, D), bf16),
         in_specs=[any_space, any_space, any_space, in_vmem, in_vmem, in_vmem, any_space, any_space],
         out_specs=in_vmem,
         scratch_shapes=[
             vmem((2, Y, 2, F, R, D // 2), bf16),
             vmem((T, D), bf16), vmem((T, D), bf16), vmem((T, D), bf16), vmem((T, D), bf16),
             vmem((2, half_units, D), bf16), vmem((half_units, D), bf16),
-            vmem((slots, T), bf16), vmem((T, slots), bf16), vmem((T, slots), bf16),
-            vmem((T, experts), f32), vmem((T, experts), f32),
+            vmem((slots, T), bf16), vmem((E // chunk, 2 * T, chunk * pairs * cap), bf16),
+            vmem((T, experts), f32), vmem((T, experts), f32), vmem((T, D), f32),
             vmem((max(slots, rows), J, 128), f32),
             vmem((experts, cap, J, 128), bf16),
             vmem((E, 2, pairs, cap, J, 128), bf16),
             vmem((rows, D), bf16), vmem((rows, half_units), bf16),
             vmem((E, 2, pairs, cap, J, 128), bf16),
             vmem((E, pairs, cap, J, 128), bf16),
-            vmem((experts, cap, J, 128), bf16),
+            vmem((E, pairs, cap, J, 128), bf16),
             dma((6,)), dma((4,)), dma, dma((N,)), dma, dma((N * N,)), dma((2,)), dma((2,)),
-            dma, dma((E,)), dma, dma((E,)), dma, dma((E,)), dma, dma,
+            dma, dma((E,)), dma, dma((E,)), dma, dma((E,)), dma, dma((E,)),
         ],
         compiler_params=pltpu.CompilerParams(
             collective_id=0, has_side_effects=True, vmem_limit_bytes=56 * 1024 * 1024

time: 169 us -> 155 us (0.917)
  Pallas kernels: 166 us -> 154 us
    pallas_call x1, Pallas kernels: 166 us -> 154 us  [on_device(): pl.pallas_call(functools.partial(block_kernel, (E, F, cap, chunk)), out_s...]
where the time goes in v2:
time: 155 us
  Pallas kernels  154 us (99%)
    pallas_call x1, Pallas kernels, on_device(): pl.pallas_call(functools.partial(block_kernel, (E, F, cap, chunk)), out_s...  154 us

profile of v2, /device:TPU:518, one launch (start us, length us, event | category | flops | bytes accessed | tf_op | source)
XLA Modules:
  0.0 154.9 jit_solution(10236540120576245576)
XLA Ops:
  0.0 154.1 %block.1 = bf16[128,2048]{1,0:T(8,128)(2,1)S(1)} custom-call(bf16[128,2048]{1,0:T(8,128)(2,1)} %tokens_hbm.1, bf16[128,2048]{1,0:T(8,128)(2,1)} %context_hbm.1, bf16[16,2048]{1,0:T(8,128)(2,1)} %shard_hbm.1, f32[1,2048]{1,0:T(1,128)} %bitcast.4, bf16[64,2048]{1,0:T(8,128)(2,1)} %bitcast.3, s32[2,128]{1,0:T(2,128)} %bitcast.5, ...), custom_call_target="tpu_custom_call" | custom-call | tf_op jit(solution)/shard_map/block/pallas_call | solution.py:433
  154.1 0.8 copy.10

commit v3 on v2

--- a/solution.py
+++ b/solution.py
@@ -144,11 +144,11 @@
     mask0[...] = jnp.transpose(one0)
     mask1[...] = jnp.transpose(one1)
 
-    def pass_on(o, step):
+    def pass_on(o, step, last):
         p1 = rem(pos1 + (o // 2 if o % 2 == 0 else N - (o + 1) // 2), N)
         for way in range(2):
             hops = N // 2 if way == o % 2 else N // 2 - 1
-            if step > hops:
+            if step > hops or last != (step == hops):
                 continue
             p2 = rem(pos2 + (N - step if way == 0 else step), N)
             ring2(way, step - 1, p1, p2, o).wait_recv()
@@ -156,7 +156,7 @@
                 ring2(way, step, p1, p2, o).start()
             to_partner(p1, p2, 1).start()
 
-    for slot in range(1, N + 1):
+    for slot in range(1, N + 1 + 1):
         if slot <= N // 2:
             for way in range(2):
                 if way == 1 and slot == N // 2:
@@ -169,10 +169,14 @@
                 ring2(0, 0, p1, pos2, o).start()
                 ring2(1, 0, p1, pos2, o).start()
                 to_partner(p1, pos2, 0).start()
+        for o in range(N - 1, -1, -1):
+            step = slot - (o + 1) // 2
+            if 1 <= step < N // 2:
+                pass_on(o, step, False)
         for o in range(N):
-            step = slot - (o + 1) // 2
-            if 1 <= step <= N // 2:
-                pass_on(o, step)
+            step = slot - 1 - (o + 1) // 2
+            if N // 2 - 1 <= step <= N // 2:
+                pass_on(o, step, True)
 
     loads[2].wait()
     loads[3].wait()
@@ -360,24 +364,6 @@
     loads[5].wait()
     groups = E // chunk
 
-    def go_back(k, carry):
-        half_back(k).start()
-        return carry
-
-    pump_first()
-    pump(1)
-    for g in range(groups):
-        if g + 2 < groups:
-            pump(g + 2)
-        experts_on(g)
-        if g == groups - 1:
-            lax.fori_loop(0, chunk, go_back, 0)
-        if g > 1:
-            finish(g - 1)
-
-    finish(groups - 1)
-    finish_first()
-
     def widen(k):
         wide[pl.ds(rem(k, chunk) * pairs * cap, pairs * cap)] = finished[k].reshape(pairs * cap, J, 128).astype(f32)
 
@@ -386,7 +372,7 @@
         widen(k)
         return carry
 
-    for g in list(range(1, groups)) + [0]:
+    def combine(g):
         if g == 0:
             wait_bytes(finished.at[0, pl.ds(0, pairs - 1)], home_recv.at[0])
             widen(0)
@@ -401,6 +387,29 @@
                 total[:, cols] = so_far
             else:
                 out_ref[:, cols] = so_far.astype(bf16)
+
+
+    def go_back(k, carry):
+        half_back(k).start()
+        return carry
+
+    pump_first()
+    pump(1)
+    for g in range(groups):
+        if g + 2 < groups:
+            pump(g + 2)
+        experts_on(g)
+        if g == groups - 1:
+            lax.fori_loop(0, chunk, go_back, 0)
+        if g > 1:
+            finish(g - 1)
+
+    finish(groups - 1)
+    for g in range(1, groups - 1):
+        combine(g)
+    finish_first()
+    combine(groups - 1)
+    combine(0)
 
     swap.wait_send()
     own.wait_send()

time: 155 us -> 150 us (0.968)
  Pallas kernels: 154 us -> 149 us
    pallas_call x1, Pallas kernels: 154 us -> 149 us  [on_device(): pl.pallas_call(functools.partial(block_kernel, (E, F, cap, chunk)), out_s...]
where the time goes in v3:
time: 150 us
  Pallas kernels  149 us (99%)
    pallas_call x1, Pallas kernels, on_device(): pl.pallas_call(functools.partial(block_kernel, (E, F, cap, chunk)), out_s...  149 us

profile of v3, /device:TPU:518, one launch (start us, length us, event | category | flops | bytes accessed | tf_op | source)
XLA Modules:
  0.0 149.6 jit_solution(15395246233998780508)
XLA Ops:
  0.0 148.8 %block.1 = bf16[128,2048]{1,0:T(8,128)(2,1)S(1)} custom-call(bf16[128,2048]{1,0:T(8,128)(2,1)} %tokens_hbm.1, bf16[128,2048]{1,0:T(8,128)(2,1)} %context_hbm.1, bf16[16,2048]{1,0:T(8,128)(2,1)} %shard_hbm.1, f32[1,2048]{1,0:T(1,128)} %bitcast.4, bf16[64,2048]{1,0:T(8,128)(2,1)} %bitcast.3, s32[2,128]{1,0:T(2,128)} %bitcast.5, ...), custom_call_target="tpu_custom_call" | custom-call | tf_op jit(solution)/shard_map/block/pallas_call | solution.py:442
  148.8 0.8 copy.10

commit v4 on v3

--- a/solution.py
+++ b/solution.py
@@ -383,7 +383,7 @@
             picked = jnp.dot(picks[g], got, preferred_element_type=f32)
             so_far = resid[:, cols].astype(f32) if g == 1 else total[:, cols]
             so_far = so_far + gate0 * picked[:T] + gate1 * picked[T:]
-            if g > 0:
+            if g < groups - 1:
                 total[:, cols] = so_far
             else:
                 out_ref[:, cols] = so_far.astype(bf16)
@@ -394,22 +394,22 @@
         return carry
 
     pump_first()
-    pump(1)
-    for g in range(groups):
-        if g + 2 < groups:
-            pump(g + 2)
+    for g in range(1, groups):
+        pump(g)
+    experts_on(0)
+    experts_on(1)
+    for g in range(2, groups):
         experts_on(g)
         if g == groups - 1:
             lax.fori_loop(0, chunk, go_back, 0)
-        if g > 1:
-            finish(g - 1)
+        finish(g - 1)
 
     finish(groups - 1)
     for g in range(1, groups - 1):
         combine(g)
     finish_first()
+    combine(0)
     combine(groups - 1)
-    combine(0)
 
     swap.wait_send()
     own.wait_send()

time: 150 us -> 150 us (level)
  no operation moved by 1% of the time
where the time goes in v4:
time: 150 us
  Pallas kernels  150 us (100%)
    pallas_call x1, Pallas kernels, on_device(): pl.pallas_call(functools.partial(block_kernel, (E, F, cap, chunk)), out_s...  150 us

profile of v4, /device:TPU:518, one launch (start us, length us, event | category | flops | bytes accessed | tf_op | source)
XLA Modules:
  0.0 150.3 jit_solution(259005527205454811)
XLA Ops:
  0.0 149.5 %block.1 = bf16[128,2048]{1,0:T(8,128)(2,1)S(1)} custom-call(bf16[128,2048]{1,0:T(8,128)(2,1)} %tokens_hbm.1, bf16[128,2048]{1,0:T(8,128)(2,1)} %context_hbm.1, bf16[16,2048]{1,0:T(8,128)(2,1)} %shard_hbm.1, f32[1,2048]{1,0:T(1,128)} %bitcast.4, bf16[64,2048]{1,0:T(8,128)(2,1)} %bitcast.3, s32[2,128]{1,0:T(2,128)} %bitcast.5, ...), custom_call_target="tpu_custom_call" | custom-call | tf_op jit(solution)/shard_map/block/pallas_call | solution.py:442
  149.5 0.8 copy.10
